TPU v7x, 32 devices: a whole 2x2x4 slice. The times are simulated.
32 devices in a mesh: grp: 2 (over y), row: 8 (over z, x), col: 1, ch: 2 (over core).
Axes of the slice: x: 2, y: 2, z: 4, core: 2. Of those that a mesh axis runs over, the one named last changes fastest.
Arguments:
- pair_act: bfloat16 [128, 256, 128], P('ch', ('grp', 'row'), 'col'), parts along dimension 1, may hold values from -48 to 48
- in_gain: float32 [128], P('ch'), may hold values from 0.1 to 1.9
- left_proj: bfloat16 [128, 128], P(None, 'ch'), may hold values from -0.5 to 0.5
- left_gate: bfloat16 [128, 128], P(None, 'ch'), may hold values from -0.5 to 0.5
- right_proj: bfloat16 [128, 128], P(None, 'ch'), may hold values from -0.5 to 0.5
- right_gate: bfloat16 [128, 128], P(None, 'ch'), may hold values from -0.5 to 0.5
- out_gate: bfloat16 [128, 128], P(None, 'ch'), may hold values from -0.5 to 0.5
- out_gain: float32 [128], P('ch'), may hold values from 0.1 to 1.9
- out_proj: bfloat16 [128, 128], P(None, 'ch'), may hold values from -0.5 to 0.5
Outputs:
- update: bfloat16 [128, 256, 128], P('ch', ('grp', 'row'), 'col'), parts along dimension 1
There are 2 independent parts, one for each index of `grp`. A program takes and returns all parts, laid end to end along the dimension named above; an argument that names none is the same for every part. Nothing has to cross between parts.
All inputs are finite; a program needn't handle non-finite values.
Results may differ from a plain program's by a relative error of at most 0.0085.
Values may be sent and summed in bfloat16 or wider, within the bound.
A program may use at most 64 MiB of HBM per device.

v0:
```python
import jax
import jax.numpy as jnp
from jax import lax
from jax.sharding import PartitionSpec as P


def spread_2(value, axis, source):
    kept = jnp.where(lax.axis_index(axis) == source, value, 0).astype(value.dtype)
    return lax.psum(kept, axis)


def moments(values, channel_count):
    first_sums, squares = lax.psum(
        (jnp.sum(values, axis=0), jnp.sum(values * values, axis=0)), "ch"
    )
    average = first_sums / channel_count
    spread = squares / channel_count - average * average
    centred = values - average[None]
    return centred * lax.rsqrt(spread + 1e-05)[None]


def per_device(
    pair_act, in_gain, left_proj, left_gate, right_proj, right_gate, out_gate, out_gain, out_proj
):
    row_count = pair_act.shape[1]
    col_count = pair_act.shape[2]
    hidden = left_proj.shape[1]
    fan_out = col_count // row_count
    normed = (
        moments(pair_act.astype(jnp.float32), pair_act.shape[0] * lax.axis_size("ch"))
        * in_gain[:, None, None]
    ).astype(jnp.bfloat16)
    whole = lax.all_gather(normed, "ch", axis=0, tiled=True)
    left_weights = jnp.concatenate((left_proj, left_gate), axis=1)
    left_lifted = jnp.einsum("cxy,cn->nyx", whole, left_weights, preferred_element_type=jnp.float32)
    left_edge = (jax.nn.sigmoid(left_lifted[hidden:]) * left_lifted[:hidden]).astype(jnp.bfloat16)
    other_weights = jnp.concatenate((right_proj, right_gate, out_gate), axis=1)
    other_lifted = jnp.einsum(
        "cxy,cn->nxy", whole, other_weights, preferred_element_type=jnp.float32
    )
    right_edge = (jax.nn.sigmoid(other_lifted[hidden : 2 * hidden]) * other_lifted[:hidden]).astype(
        jnp.bfloat16
    )
    gate_map = jax.nn.sigmoid(other_lifted[2 * hidden :])
    blocks = left_edge.reshape(hidden, fan_out, row_count, row_count)
    outgoing = jnp.tile(blocks, (1, lax.axis_size("row") // fan_out, 1, 1))
    arrived = lax.all_to_all(outgoing, "row", split_axis=1, concat_axis=3, tiled=True)
    left_panel = arrived.reshape(hidden, row_count, -1)
    left_panel = spread_2(left_panel, "col", lax.axis_index("row") // fan_out)
    tri_sum = jnp.einsum(
        "hik,hkj->hij",
        left_panel,
        lax.all_gather(right_edge, "row", axis=1, tiled=True),
        preferred_element_type=jnp.float32,
    )
    mid_norm = (moments(tri_sum, hidden * lax.axis_size("ch")) * out_gain[:, None, None]).astype(
        jnp.bfloat16
    )
    all_mid = lax.all_gather(mid_norm, "ch", axis=0, tiled=True)
    projected = jnp.einsum("hxy,hc->cxy", all_mid, out_proj, preferred_element_type=jnp.float32)
    return (gate_map * projected).astype(jnp.bfloat16)


def solution(mesh):
    return jax.shard_map(
        per_device,
        mesh=mesh,
        in_specs=(
            P("ch", ("grp", "row"), "col"),
            P("ch"),
            P(None, "ch"),
            P(None, "ch"),
            P(None, "ch"),
            P(None, "ch"),
            P(None, "ch"),
            P("ch"),
            P(None, "ch"),
        ),
        out_specs=P("ch", ("grp", "row"), "col"),
        check_vma=False,
    )
```

profile of v0, /device:TPU:1, one launch (start us, length us, event | category | flops | bytes accessed | tf_op | source)
XLA Modules:
  0.0 88.1 jit_solution(10436490548046105974)
XLA Ops:
  6.5 0.0 copy-start
  6.5 0.0 all-gather.2.cloned.1.call-start
  6.5 1.1 %convert_reduce_fusion = (f32[16,128]{1,0:T(8,128)S(1)}, f32[16,128]{1,0:T(8,128)S(1)}) fusion(bf16[64,16,128]{2,1,0:T(8,128)(2,1)} %param.9), kind=kLoop, calls=%fused_computation.8 | loop fusion | flops 520192 | bytes 278528 | tf_op jit(solution)/shard_map/reduce_sum | solution.py:14
  7.6 3.3 %all-reduce.1 = (f32[16,128]{1,0:T(8,128)S(1)}, f32[16,128]{1,0:T(8,128)S(1)}) all-reduce(f32[16,128]{1,0:T(8,128)S(1)} %get-tuple-element.8, f32[16,128]{1,0:T(8,128)S(1)} %get-tuple-element.7), channel_id=1, replica_groups=mesh['grp'=2,'row'=8,'col'=1,'ch'=2] {'ch'}, use_global_device_ids=true, to_apply=%region_3.0 | all-reduce | flops 4096 | bytes 32768 | tf_op jit(solution)/shard_map/psum | solution.py:13
  10.9 1.1 %fusion.6 = bf16[64,16,128]{2,0,1:T(8,128)(2,1)S(1)} fusion(f32[64]{0:T(128)} %param.10, f32[16,128]{1,0:T(8,128)S(1)} %get-tuple-element.16, f32[16,128]{1,0:T(8,128)S(1)} %get-tuple-element.15, bf16[64,16,128]{2,1,0:T(8,128)(2,1)} %param.9), kind=kLoop, calls=%fused_computation.11 | loop fusion | flops 655360 | bytes 540928 | tf_op jit(solution)/shard_map/convert_element_type | solution.py:32
  12.0 0.0 copy-start.1
  12.0 0.0 copy-start.2
  12.0 2.2 %all_gather.9 = bf16[128,16,128]{2,0,1:T(8,128)(2,1)S(1)} all-gather(bf16[64,16,128]{2,0,1:T(8,128)(2,1)S(1)} %fusion.6), channel_id=1, replica_groups=mesh['grp'=2,'row'=8,'col'=1,'ch'=2] {'ch'}, dimensions={0}, use_global_device_ids=true | all-gather | bytes 786432 | tf_op jit(solution)/shard_map/all_gather | solution.py:33
  14.2 1.1 %fusion.20 = f32[192,16,128]{2,0,1:T(8,128)S(1)} fusion(bf16[128,16,128]{2,0,1:T(8,128)(2,1)S(1)} %all_gather.9, bf16[128,64]{0,1:T(8,128)(2,1)} %param.15, bf16[128,64]{0,1:T(8,128)(2,1)} %param.14, bf16[128,64]{0,1:T(8,128)(2,1)} %param.13), kind=kOutput, calls=%fused_computation.34 | convolution fusion | flops 100810752 | bytes 2146304 | tf_op jit(solution)/shard_map/cxy,cn->nxy/dot_general | solution.py:38
  15.3 0.9 fusion.8
  16.2 0.0 all-gather.2.cloned.1.call-update
  16.2 0.0 copy-done.1
  16.2 0.0 copy-done.2
  16.2 0.3 convolution_bitcast_fusion
  16.5 0.1 fusion.12
  16.7 0.4 copy.23
  17.1 1.1 %reshape.17 = bf16[8,2,8192]{2,1,0:T(2,128)(2,1)} reshape(bf16[8,16,16,64]{3,2,1,0:T(8,128)(2,1)S(1)} %bitcast.29) | data formatting | bytes 524288
  18.2 6.8 %all-to-all-start = ((bf16[8,2,8192]{2,1,0:T(2,128)(2,1)}), bf16[8,2,8192]{2,1,0:T(2,128)(2,1)S(1)}, u32[]{:S(2)}, u32[]{:S(2)}) async-start(bf16[8,2,8192]{2,1,0:T(2,128)(2,1)} %reshape.17), calls=%async_computation | async-start | bytes 524288 | tf_op jit(solution)/shard_map/all_to_all | solution.py:47
  25.1 8.9 %all-to-all-done = bf16[8,2,8192]{2,1,0:T(2,128)(2,1)S(1)} async-done(((bf16[8,2,8192]{2,1,0:T(2,128)(2,1)}), bf16[8,2,8192]{2,1,0:T(2,128)(2,1)S(1)}, u32[]{:S(2)}, u32[]{:S(2)}) %all-to-all-start) | async-done | bytes 262176 | tf_op jit(solution)/shard_map/all_to_all | solution.py:47
  33.9 0.3 reshape.18
  34.4 0.0 copy-start.3
  34.4 0.3 copy.25
  34.7 33.9 %all-gather.2.cloned.1.call-done = bf16[64,128,128]{2,0,1:T(8,128)(2,1)} async-done(((bf16[64,16,128]{2,0,1:T(8,128)(2,1)}), bf16[64,128,128]{2,0,1:T(8,128)(2,1)}) %all-gather.2.cloned.1.call-update) | async-done | bytes 2097168 | tf_op jit(solution)/shard_map/all_gather | solution.py:53
  68.6 3.5 %fusion.30 = (f32[16,128]{1,0:T(8,128)S(1)}, f32[16,128]{1,0:T(8,128)S(1)}, f32[64,16,128]{2,1,0:T(8,128)S(1)}) fusion(bf16[64,16,128]{2,1,0:T(8,128)(2,1)S(1)} %copy.25, bf16[64,128,128]{2,0,1:T(8,128)(2,1)} %all-gather.2.cloned.1.call-done), kind=kOutput, calls=%fused_computation.49 | convolution fusion | flops 33943552 | bytes 2899968 | tf_op jit(solution)/shard_map/hik,hkj->hij/dot_general | solution.py:50
  72.1 5.7 %all-reduce = (f32[16,128]{1,0:T(8,128)S(1)}, f32[16,128]{1,0:T(8,128)S(1)}) all-reduce(f32[16,128]{1,0:T(8,128)S(1)} %get-tuple-element.6, f32[16,128]{1,0:T(8,128)S(1)} %get-tuple-element.5), channel_id=1, replica_groups=mesh['grp'=2,'row'=8,'col'=1,'ch'=2] {'ch'}, use_global_device_ids=true, to_apply=%region_7.8 | all-reduce | flops 4096 | bytes 32768 | tf_op jit(solution)/shard_map/psum | solution.py:13
  77.8 0.0 copy-done.3
  77.8 0.1 multiply_convert_fusion
  78.0 2.2 %all_gather.11 = bf16[128,16,128]{2,1,0:T(8,128)(2,1)S(1)} all-gather(bf16[64,16,128]{2,1,0:T(8,128)(2,1)S(1)} %multiply_convert_fusion), channel_id=1, replica_groups=mesh['grp'=2,'row'=8,'col'=1,'ch'=2] {'ch'}, dimensions={0}, use_global_device_ids=true | all-gather | bytes 786432 | tf_op jit(solution)/shard_map/all_gather | solution.py:59
  80.1 0.0 copy-done
  80.1 0.3 fusion.3
  80.4 0.9 copy.28
  (4 shorter events, 0.1 us)
Async XLA Ops:
  6.5 73.6 %copy-start = (bf16[128,64]{0,1:T(8,128)(2,1)S(1)}, bf16[128,64]{0,1:T(8,128)(2,1)}, u32[]{:S(2)}) copy-start(bf16[128,64]{0,1:T(8,128)(2,1)} %param.17) | copy-start | bytes 49156
  6.5 62.1 %all-gather.2.cloned.1.call-start = ((), (), s32[]{:S(2)}) async-start(), calls=%async_computation.1 | async-start | bytes 2359296 | tf_op jit(solution)/shard_map/all_gather | solution.py:53
  12.0 4.2 %copy-start.1 = (bf16[128,64]{0,1:T(8,128)(2,1)S(1)}, bf16[128,64]{0,1:T(8,128)(2,1)}, u32[]{:S(2)}) copy-start(bf16[128,64]{0,1:T(8,128)(2,1)} %param.12) | copy-start | bytes 49156
  12.0 4.2 %copy-start.2 = (bf16[128,64]{0,1:T(8,128)(2,1)S(1)}, bf16[128,64]{0,1:T(8,128)(2,1)}, u32[]{:S(2)}) copy-start(bf16[128,64]{0,1:T(8,128)(2,1)} %param.11) | copy-start | bytes 49156
  18.2 15.7 %all-to-all-start = ((bf16[8,2,8192]{2,1,0:T(2,128)(2,1)}), bf16[8,2,8192]{2,1,0:T(2,128)(2,1)S(1)}, u32[]{:S(2)}, u32[]{:S(2)}) async-start(bf16[8,2,8192]{2,1,0:T(2,128)(2,1)} %reshape.17), calls=%async_computation | async-start | bytes 524288 | tf_op jit(solution)/shard_map/all_to_all | solution.py:47
  34.4 43.4 %copy-start.3 = (f32[64]{0:T(128)S(1)}, f32[64]{0:T(128)}, u32[]{:S(2)}) copy-start(f32[64]{0:T(128)} %param.16) | copy-start | bytes 772
Sparse Core Ops, SparseCore 0:
  16.3 52.2 all-gather.1
where the time goes:
time: 88.7 us; the launch traced here: 88.1 us
  waiting for transfers between devices  42.8 us (48%)
  between operations  13.5 us (15%)
  blocking collectives  13.4 us (15%)
  starting transfers between devices  6.85 us (8%)
  matrix products  5.09 us (6%)
  other arithmetic  3.38 us (4%)
  local copies, waits for them, and re-layouts  3.09 us (3%)
    all_gather x1, waiting for transfers between devices, per_device(): lax.all_gather(right_edge, 'row', axis=1, tiled=True)  33.9 us
    psum x2, blocking collectives, moments(): lax.psum((jnp.sum(values, axis=0), jnp.sum(values * values, axis=0)), 'ch')  9 us
    all_to_all x1, waiting for transfers between devices, per_device(): lax.all_to_all(outgoing, 'row', split_axis=1, concat_axis=3, tiled=True)  8.88 us
    all_to_all x1, starting transfers between devices, per_device(): lax.all_to_all(outgoing, 'row', split_axis=1, concat_axis=3, tiled=True)  6.85 us
    dot_general x1, matrix products, per_device(): jnp.einsum('hik,hkj->hij', left_panel, lax.all_gather(right_edge, 'row',...  3.46 us
    all_gather x1, blocking collectives, per_device(): whole = lax.all_gather(normed, 'ch', axis=0, tiled=True)  2.18 us
    all_gather x1, blocking collectives, per_device(): all_mid = lax.all_gather(mid_norm, 'ch', axis=0, tiled=True)  2.18 us
  transfers between devices with their start and end apart: 2, of which 2 were waited for; matrix products, arithmetic and copies ran while one was open for 3% of the time, Pallas kernels for 0%

commit v1 on v0

--- a/solution.py
+++ b/solution.py
@@ -1,6 +1,10 @@
+import functools
+
 import jax
 import jax.numpy as jnp
 from jax import lax
+from jax.experimental import pallas as pl
+from jax.experimental.pallas import tpu as pltpu
 from jax.sharding import PartitionSpec as P
 
 
@@ -61,9 +65,278 @@
     return (gate_map * projected).astype(jnp.bfloat16)
 
 
+MESH = pl.DeviceIdType.MESH
+
+
+def swap_major(values):
+    return jnp.swapaxes(values, 0, 1)
+
+
+def spread_gain(gain, lanes):
+    return jnp.broadcast_to(gain, (lanes, gain.shape[1])).T
+
+
+def centred_unit(values):
+    count = values.shape[0]
+    average = jnp.sum(values, axis=0) / count
+    centred = values - average[None]
+    spread = jnp.sum(centred * centred, axis=0) / count
+    return centred * lax.rsqrt(spread + 1e-05)[None]
+
+
+def fused_kernel(
+    rows,
+    act_ref,
+    gain_ref,
+    lp_ref,
+    lg_ref,
+    rp_ref,
+    rg_ref,
+    og_ref,
+    gain2_ref,
+    op_ref,
+    out_ref,
+    raw,
+    gains,
+    weights,
+    normed,
+    gates,
+    outbox,
+    inbox,
+    edges,
+    tri_out,
+    mid,
+    load_sem,
+    pair_send,
+    pair_recv,
+    lr_send,
+    lr_recv,
+    tri_send,
+    tri_recv,
+    relay_send,
+    relay_recv,
+):
+    me = lax.axis_index("row")
+    core = lax.axis_index("ch")
+    other = 1 - core
+    half, depth, width = act_ref.shape
+    hidden = lp_ref.shape[0]
+    block = hidden // rows
+    partner = {"ch": other}
+    peers = [lax.rem(me + d, rows) for d in range(rows)]
+    sources = [lax.rem(me + rows - d, rows) for d in range(rows)]
+
+    loads = [pltpu.make_async_copy(act_ref, raw.at[core], load_sem.at[0])]
+    for n, ref in enumerate((lp_ref, lg_ref, rp_ref, rg_ref, og_ref, op_ref)):
+        loads.append(
+            pltpu.make_async_copy(
+                ref, weights.at[pl.ds(n * hidden, hidden)], load_sem.at[n + 1]
+            )
+        )
+    for load in loads:
+        load.start()
+    barrier = pltpu.get_barrier_semaphore()
+    pl.semaphore_signal(barrier, inc=1, device_id=partner, device_id_type=MESH)
+    for d in range(1, rows):
+        pl.semaphore_signal(barrier, inc=1, device_id={"row": peers[d]}, device_id_type=MESH)
+    gains[core, 0] = spread_gain(gain_ref[...], width)
+    gains[core, 1] = spread_gain(gain2_ref[...], width)
+    loads[0].wait()
+    pl.semaphore_wait(barrier, rows)
+
+    def to_partner(ref, n):
+        return pltpu.make_async_remote_copy(
+            src_ref=ref,
+            dst_ref=ref,
+            send_sem=pair_send.at[n],
+            recv_sem=pair_recv.at[n],
+            device_id=partner,
+            device_id_type=MESH,
+        )
+
+    swaps = [to_partner(raw.at[core], 0), to_partner(gains.at[core], 1)]
+    for swap in swaps:
+        swap.start()
+    for load in loads[1:]:
+        load.wait()
+    for swap in swaps:
+        swap.wait_recv()
+
+    in_gain = gains[:, 0].reshape(2 * half, width)
+    edge_weights = weights[pl.ds(0, 4 * hidden)]
+    step = 8
+    for start in range(0, depth, step):
+        values = raw[:, :, pl.ds(start, step)].astype(jnp.float32)
+        turned = swap_major(centred_unit(values.reshape(2 * half, step, width)))
+        for x in range(step):
+            operand = (turned[x] * in_gain).astype(jnp.bfloat16)
+            normed[start + x] = operand
+            lifted = jnp.dot(edge_weights, operand, preferred_element_type=jnp.float32)
+            left = jax.nn.sigmoid(lifted[hidden : 2 * hidden]) * lifted[:hidden]
+            right = jax.nn.sigmoid(lifted[3 * hidden :]) * lifted[2 * hidden : 3 * hidden]
+            both = jnp.concatenate(
+                (left.reshape(rows, block, width), right.reshape(rows, block, width)), axis=1
+            )
+            outbox[:, start + x] = both.astype(jnp.bfloat16)
+
+    def to_peer(src, dst, d, sends, recvs):
+        return pltpu.make_async_remote_copy(
+            src_ref=src,
+            dst_ref=dst,
+            send_sem=sends.at[d],
+            recv_sem=recvs.at[d],
+            device_id={"row": peers[d]},
+            device_id_type=MESH,
+        )
+
+    edge_copies = {
+        d: to_peer(outbox.at[peers[d]], inbox.at[me], d, lr_send, lr_recv) for d in range(1, rows)
+    }
+    for copy in edge_copies.values():
+        copy.start()
+
+    def take_edges(box, source):
+        turned = swap_major(box.astype(jnp.float32)).astype(jnp.bfloat16)
+        edges[:, pl.ds(pl.multiple_of(source * depth, depth), depth)] = turned
+
+    take_edges(outbox[me], me)
+    gate_weights = weights[pl.ds(4 * hidden, hidden)]
+    for x in range(depth):
+        gates[x] = jax.nn.sigmoid(
+            jnp.dot(gate_weights, normed[x], preferred_element_type=jnp.float32)
+        )
+    for d in range(1, rows):
+        edge_copies[d].wait_recv()
+        take_edges(inbox[sources[d]], sources[d])
+
+    for h in range(block):
+        tri_sum = lax.dot_general(
+            edges[h],
+            edges[block + h],
+            (((0,), (0,)), ((), ())),
+            preferred_element_type=jnp.float32,
+        )
+        tri_out[:, h] = tri_sum.astype(jnp.bfloat16).reshape(rows, depth, width)
+
+    tri_copies = {
+        d: to_peer(tri_out.at[peers[d]], mid.at[core, me], d, tri_send, tri_recv)
+        for d in range(1, rows)
+    }
+    for copy in tri_copies.values():
+        copy.start()
+    mid[core, me] = tri_out[me]
+
+    def relay(source, n, ref):
+        return pltpu.make_async_remote_copy(
+            src_ref=ref,
+            dst_ref=mid.at[core, source],
+            send_sem=relay_send.at[n],
+            recv_sem=relay_recv.at[n],
+            device_id=partner,
+            device_id_type=MESH,
+        )
+
+    relays = [relay(me, 0, tri_out.at[me])]
+    relays[0].start()
+    for d in range(1, rows):
+        tri_copies[d].wait_recv()
+        relays.append(relay(sources[d], d, mid.at[core, sources[d]]))
+        relays[d].start()
+    for copy in relays:
+        copy.wait_recv()
+
+    out_gain = gains[:, 1].reshape(2 * half, width)
+    out_weights = weights[pl.ds(5 * hidden, hidden)]
+    for start in range(0, depth, step):
+        values = mid[:, :, :, pl.ds(start, step)].astype(jnp.float32)
+        turned = swap_major(centred_unit(values.reshape(2 * hidden, step, width)))
+        updates = []
+        for x in range(step):
+            operand = (turned[x] * out_gain).astype(jnp.bfloat16)
+            projected = jnp.dot(out_weights, operand, preferred_element_type=jnp.float32)
+            updates.append((gates[start + x] * projected)[None])
+        stacked = swap_major(jnp.concatenate(updates, axis=0))
+        out_ref[:, pl.ds(start, step)] = stacked.astype(jnp.bfloat16)
+
+    for swap in swaps:
+        swap.wait_send()
+    for copy in (*edge_copies.values(), *tri_copies.values(), *relays):
+        copy.wait_send()
+
+
+def fused_device(
+    rows, pair_act, in_gain, left_proj, left_gate, right_proj, right_gate, out_gate, out_gain, out_proj
+):
+    half, depth, width = pair_act.shape
+    hidden = left_proj.shape[1]
+    block = hidden // rows
+    channels = 2 * half
+    anywhere = pl.BlockSpec(memory_space=pl.ANY)
+    local = pl.BlockSpec(memory_space=pltpu.VMEM)
+    bf16 = jnp.bfloat16
+    dma = pltpu.SemaphoreType.DMA
+    return pl.pallas_call(
+        functools.partial(fused_kernel, rows),
+        out_shape=jax.ShapeDtypeStruct(pair_act.shape, bf16),
+        in_specs=[anywhere, local] + [anywhere] * 5 + [local, anywhere],
+        out_specs=local,
+        scratch_shapes=[
+            pltpu.VMEM((2, half, depth, width), bf16),
+            pltpu.VMEM((2, 2, half, width), jnp.float32),
+            pltpu.VMEM((6 * hidden, channels), bf16),
+            pltpu.VMEM((depth, channels, width), bf16),
+            pltpu.VMEM((depth, hidden, width), jnp.float32),
+            pltpu.VMEM((rows, depth, 2 * block, width), bf16),
+            pltpu.VMEM((rows, depth, 2 * block, width), bf16),
+            pltpu.VMEM((2 * block, rows * depth, width), bf16),
+            pltpu.VMEM((rows, block, depth, width), bf16),
+            pltpu.VMEM((2, rows, block, depth, width), bf16),
+            dma((7,)),
+            dma((2,)),
+            dma((2,)),
+            dma((rows,)),
+            dma((rows,)),
+            dma((rows,)),
+            dma((rows,)),
+            dma((rows,)),
+            dma((rows,)),
+        ],
+        compiler_params=pltpu.CompilerParams(collective_id=0, has_side_effects=True),
+        name="triangle",
+    )(
+        pair_act,
+        in_gain[None],
+        left_proj.T,
+        left_gate.T,
+        right_proj.T,
+        right_gate.T,
+        out_gate.T,
+        out_gain[None],
+        out_proj.T,
+    )
+
+
+def dispatch(sizes, *args):
+    half, depth, width = args[0].shape
+    hidden = args[2].shape[1]
+    rows = sizes["row"]
+    fits = (
+        sizes["col"] == 1
+        and sizes["ch"] == 2
+        and width == rows * depth
+        and half == hidden
+        and hidden % (8 * rows) == 0
+        and depth % 16 == 0
+        and width % 128 == 0
+    )
+    if fits:
+        return fused_device(rows, *args)
+    return per_device(*args)
+
+
 def solution(mesh):
     return jax.shard_map(
-        per_device,
+        functools.partial(dispatch, dict(mesh.shape)),
         mesh=mesh,
         in_specs=(
             P("ch", ("grp", "row"), "col"),

time: 88.7 us -> 32.6 us (0.37)
  waiting for transfers between devices: 42.8 us -> 0 us
  Pallas kernels: 0 us -> 30.8 us
  between operations: 13.5 us -> 0.01 us
  blocking collectives: 13.4 us -> 0 us
  starting transfers between devices: 6.85 us -> 0 us
  matrix products: 5.09 us -> 0 us
  other arithmetic: 3.38 us -> 0 us
  local copies, waits for them, and re-layouts: 3.09 us -> 1.67 us
    all_gather x1 -> x0, waiting for transfers between devices: 33.9 us -> none  [per_device(): lax.all_gather(right_edge, 'row', axis=1, tiled=True)]
    pallas_call x0 -> x1, Pallas kernels: none -> 30.8 us  [fused_device(): pl.pallas_call(functools.partial(fused_kernel, rows), out_shape=jax.Shape...]
    psum x2 -> x0, blocking collectives: 9 us -> none  [moments(): lax.psum((jnp.sum(values, axis=0), jnp.sum(values * values, axis=0)), 'ch')]
    all_to_all x1 -> x0, waiting for transfers between devices: 8.88 us -> none  [per_device(): lax.all_to_all(outgoing, 'row', split_axis=1, concat_axis=3, tiled=True)]
    all_to_all x1 -> x0, starting transfers between devices: 6.85 us -> none  [per_device(): lax.all_to_all(outgoing, 'row', split_axis=1, concat_axis=3, tiled=True)]
    dot_general x4 -> x0, matrix products: 5.09 us -> none  [the longest x1 3.46 us: per_device(): jnp.einsum('hik,hkj->hij', left_panel, lax.all_gather(right_edge, 'row',...]
    all_gather x2 -> x0, blocking collectives: 4.36 us -> none  [the longest x1 2.18 us: per_device(): whole = lax.all_gather(normed, 'ch', axis=0, tiled=True)]
    convert_element_type x4 -> x0, other arithmetic: 2.25 us -> none  [the longest x1 1.09 us: per_device(): normed = (moments(pair_act.astype(jnp.float32), pair_act.shape[0] * lax.a...]
  transfers between devices with their start and end apart: 2 -> 0, of which waited for: 2 -> 0; matrix products, arithmetic and copies ran while one was open for 3% -> 0% of each run, Pallas kernels for 0% -> 0%
where the time goes in v1:
time: 32.6 us; the launch traced here: 32.5 us
  Pallas kernels  30.8 us (94%)
  local copies, waits for them, and re-layouts  1.67 us (5%)
    pallas_call x1, Pallas kernels, fused_device(): pl.pallas_call(functools.partial(fused_kernel, rows), out_shape=jax.Shape...  30.8 us
    unnamed x1, local copies, waits for them, and re-layouts  1.67 us

profile of v1, /device:TPU:1, one launch (start us, length us, event | category | flops | bytes accessed | tf_op | source)
XLA Modules:
  0.0 32.5 jit_solution(7115315214292381252)
XLA Ops:
  0.0 30.8 %triangle.1 = bf16[64,16,128]{2,1,0:T(8,128)(2,1)} custom-call(bf16[64,16,128]{2,1,0:T(8,128)(2,1)} %act_ref.1, f32[1,64]{1,0:T(1,128)} %bitcast.14, bf16[64,128]{1,0:T(8,128)(2,1)} %bitcast.8, bf16[64,128]{1,0:T(8,128)(2,1)} %bitcast.9, bf16[64,128]{1,0:T(8,128)(2,1)} %bitcast.10, bf16[64,128]{1,0:T(8,128)(2,1)} %bitcast.11, bf16[64,128]{1,0:T(8,128)(2,1)} %bitcast.12, ...), custom_call_target="tpu_custom_call" | custom-call | tf_op jit(solution)/shard_map/triangle/pallas_call | solution.py:278
  30.8 1.7 %copy.11 = bf16[64,16,128]{2,1,0:T(8,128)(2,1)} copy(bf16[64,16,128]{2,1,0:T(8,128)(2,1)} %triangle.1) | data formatting | bytes 524288

commit v2 on v1

--- a/solution.py
+++ b/solution.py
@@ -76,12 +76,12 @@
     return jnp.broadcast_to(gain, (lanes, gain.shape[1])).T
 
 
-def centred_unit(values):
+def centred_unit(values, gain):
     count = values.shape[0]
-    average = jnp.sum(values, axis=0) / count
-    centred = values - average[None]
-    spread = jnp.sum(centred * centred, axis=0) / count
-    return centred * lax.rsqrt(spread + 1e-05)[None]
+    average = jnp.sum(values, axis=0, keepdims=True) / count
+    centred = values - average
+    spread = jnp.sum(centred * centred, axis=0, keepdims=True) / count
+    return (centred * lax.rsqrt(spread + 1e-05) * gain).astype(jnp.bfloat16)
 
 
 def fused_kernel(
@@ -97,14 +97,17 @@
     op_ref,
     out_ref,
     raw,
+    act,
     gains,
     weights,
+    edge_weights,
     normed,
     gates,
     outbox,
     inbox,
     edges,
     tri_out,
+    tri_in,
     mid,
     load_sem,
     pair_send,
@@ -121,18 +124,17 @@
     other = 1 - core
     half, depth, width = act_ref.shape
     hidden = lp_ref.shape[0]
-    block = hidden // rows
+    part = hidden // rows // 2
     partner = {"ch": other}
     peers = [lax.rem(me + d, rows) for d in range(rows)]
     sources = [lax.rem(me + rows - d, rows) for d in range(rows)]
-
-    loads = [pltpu.make_async_copy(act_ref, raw.at[core], load_sem.at[0])]
+    order = sorted(range(1, rows), key=lambda d: -min(d, rows - d))
+    step = depth // 2
+    halves = (pl.ds(0, step), pl.ds(step, step))
+
+    loads = [pltpu.make_async_copy(act_ref, raw, load_sem.at[0])]
     for n, ref in enumerate((lp_ref, lg_ref, rp_ref, rg_ref, og_ref, op_ref)):
-        loads.append(
-            pltpu.make_async_copy(
-                ref, weights.at[pl.ds(n * hidden, hidden)], load_sem.at[n + 1]
-            )
-        )
+        loads.append(pltpu.make_async_copy(ref, weights.at[n], load_sem.at[n + 1]))
     for load in loads:
         load.start()
     barrier = pltpu.get_barrier_semaphore()
@@ -142,7 +144,9 @@
     gains[core, 0] = spread_gain(gain_ref[...], width)
     gains[core, 1] = spread_gain(gain2_ref[...], width)
     loads[0].wait()
-    pl.semaphore_wait(barrier, rows)
+    for n in range(2):
+        turned = swap_major(raw[:, halves[n]].astype(jnp.float32))
+        act[core, halves[n]] = turned.astype(jnp.bfloat16)
 
     def to_partner(ref, n):
         return pltpu.make_async_remote_copy(
@@ -154,113 +158,146 @@
             device_id_type=MESH,
         )
 
-    swaps = [to_partner(raw.at[core], 0), to_partner(gains.at[core], 1)]
+    pl.semaphore_wait(barrier, rows)
+    swaps = [
+        to_partner(gains.at[core], 2),
+        to_partner(act.at[core, halves[0]], 0),
+        to_partner(act.at[core, halves[1]], 1),
+    ]
     for swap in swaps:
         swap.start()
     for load in loads[1:]:
         load.wait()
-    for swap in swaps:
-        swap.wait_recv()
-
-    in_gain = gains[:, 0].reshape(2 * half, width)
-    edge_weights = weights[pl.ds(0, 4 * hidden)]
-    step = 8
-    for start in range(0, depth, step):
-        values = raw[:, :, pl.ds(start, step)].astype(jnp.float32)
-        turned = swap_major(centred_unit(values.reshape(2 * half, step, width)))
-        for x in range(step):
-            operand = (turned[x] * in_gain).astype(jnp.bfloat16)
-            normed[start + x] = operand
-            lifted = jnp.dot(edge_weights, operand, preferred_element_type=jnp.float32)
-            left = jax.nn.sigmoid(lifted[hidden : 2 * hidden]) * lifted[:hidden]
-            right = jax.nn.sigmoid(lifted[3 * hidden :]) * lifted[2 * hidden : 3 * hidden]
-            both = jnp.concatenate(
-                (left.reshape(rows, block, width), right.reshape(rows, block, width)), axis=1
-            )
-            outbox[:, start + x] = both.astype(jnp.bfloat16)
-
-    def to_peer(src, dst, d, sends, recvs):
+    for n in range(2):
+        first = weights[n].astype(jnp.float32).reshape(rows, 2, part, 2 * half)
+        second = weights[n + 2].astype(jnp.float32).reshape(rows, 2, part, 2 * half)
+        joined = jnp.concatenate((first, second), axis=2)
+        edge_weights[n] = joined.reshape(2 * hidden, 2 * half).astype(jnp.bfloat16)
+
+    def edge_copy(n, src, dst, d):
         return pltpu.make_async_remote_copy(
             src_ref=src,
             dst_ref=dst,
-            send_sem=sends.at[d],
-            recv_sem=recvs.at[d],
+            send_sem=lr_send.at[n, d],
+            recv_sem=lr_recv.at[n, d],
             device_id={"row": peers[d]},
             device_id_type=MESH,
         )
 
-    edge_copies = {
-        d: to_peer(outbox.at[peers[d]], inbox.at[me], d, lr_send, lr_recv) for d in range(1, rows)
-    }
-    for copy in edge_copies.values():
-        copy.start()
-
-    def take_edges(box, source):
+    first_copies = [
+        {
+            d: edge_copy(n, outbox.at[0, peers[d], halves[n]], inbox.at[0, me, halves[n]], d)
+            for d in order
+        }
+        for n in range(2)
+    ]
+    last_copies = {d: edge_copy(2, outbox.at[1, peers[d]], inbox.at[1, me], d) for d in order}
+
+    swaps[0].wait_recv()
+    in_gain = gains[:, 0].reshape(2 * half, width)
+    lift_weights = edge_weights[...].reshape(4 * hidden, 2 * half)
+    for n in range(2):
+        swaps[1 + n].wait_recv()
+        for x in range(n * step, (n + 1) * step):
+            values = act[:, x].astype(jnp.float32).reshape(2 * half, width)
+            operand = centred_unit(values, in_gain)
+            normed[x] = operand
+            lifted = jnp.dot(lift_weights, operand, preferred_element_type=jnp.float32)
+            both = jax.nn.sigmoid(lifted[2 * hidden :]) * lifted[: 2 * hidden]
+            both = both.reshape(rows, 2, 2 * part, width).astype(jnp.bfloat16)
+            outbox[0, :, x] = both[:, 0]
+            outbox[1, :, x] = both[:, 1]
+        for d in order:
+            first_copies[n][d].start()
+    for d in order:
+        last_copies[d].start()
+
+    def take_edges(n, box, source):
         turned = swap_major(box.astype(jnp.float32)).astype(jnp.bfloat16)
-        edges[:, pl.ds(pl.multiple_of(source * depth, depth), depth)] = turned
-
-    take_edges(outbox[me], me)
-    gate_weights = weights[pl.ds(4 * hidden, hidden)]
+        edges[n, :, pl.ds(pl.multiple_of(source * depth, depth), depth)] = turned
+
+    for n in range(2):
+        take_edges(n, outbox[n, me], me)
+    gate_weights = weights[4]
     for x in range(depth):
         gates[x] = jax.nn.sigmoid(
             jnp.dot(gate_weights, normed[x], preferred_element_type=jnp.float32)
         )
-    for d in range(1, rows):
-        edge_copies[d].wait_recv()
-        take_edges(inbox[sources[d]], sources[d])
-
-    for h in range(block):
-        tri_sum = lax.dot_general(
-            edges[h],
-            edges[block + h],
-            (((0,), (0,)), ((), ())),
-            preferred_element_type=jnp.float32,
-        )
-        tri_out[:, h] = tri_sum.astype(jnp.bfloat16).reshape(rows, depth, width)
-
-    tri_copies = {
-        d: to_peer(tri_out.at[peers[d]], mid.at[core, me], d, tri_send, tri_recv)
-        for d in range(1, rows)
-    }
-    for copy in tri_copies.values():
-        copy.start()
-    mid[core, me] = tri_out[me]
-
-    def relay(source, n, ref):
+
+    def tri_copy(n, d):
         return pltpu.make_async_remote_copy(
-            src_ref=ref,
+            src_ref=tri_out.at[peers[d], n],
+            dst_ref=tri_in.at[me, n],
+            send_sem=tri_send.at[n, d],
+            recv_sem=tri_recv.at[n, d],
+            device_id={"row": peers[d]},
+            device_id_type=MESH,
+        )
+
+    tri_copies = [{d: tri_copy(n, d) for d in order} for n in range(2)]
+    for n in range(2):
+        for d in order:
+            if n == 0:
+                first_copies[0][d].wait_recv()
+                first_copies[1][d].wait_recv()
+            else:
+                last_copies[d].wait_recv()
+            take_edges(n, inbox[n, sources[d]], sources[d])
+        for h in range(part):
+            tri_sum = lax.dot_general(
+                edges[n, h],
+                edges[n, part + h],
+                (((0,), (0,)), ((), ())),
+                preferred_element_type=jnp.float32,
+            )
+            tri_out[:, n, h] = tri_sum.astype(jnp.bfloat16).reshape(rows, depth, width)
+        for d in order:
+            tri_copies[n][d].start()
+
+    def relay(source, d):
+        return pltpu.make_async_remote_copy(
+            src_ref=mid.at[core, source],
             dst_ref=mid.at[core, source],
-            send_sem=relay_send.at[n],
-            recv_sem=relay_recv.at[n],
+            send_sem=relay_send.at[d],
+            recv_sem=relay_recv.at[d],
             device_id=partner,
             device_id_type=MESH,
         )
 
-    relays = [relay(me, 0, tri_out.at[me])]
+    def take_mid(block, source):
+        block = block.astype(jnp.float32).reshape(2 * part, depth, width)
+        mid[core, source] = swap_major(block).astype(jnp.bfloat16)
+
+    take_mid(tri_out[me], me)
+    relays = [relay(me, 0)]
     relays[0].start()
-    for d in range(1, rows):
-        tri_copies[d].wait_recv()
-        relays.append(relay(sources[d], d, mid.at[core, sources[d]]))
-        relays[d].start()
+    for d in order:
+        for n in range(2):
+            tri_copies[n][d].wait_recv()
+        take_mid(tri_in[sources[d]], sources[d])
+        relays.append(relay(sources[d], d))
+        relays[-1].start()
     for copy in relays:
         copy.wait_recv()
 
     out_gain = gains[:, 1].reshape(2 * half, width)
-    out_weights = weights[pl.ds(5 * hidden, hidden)]
+    out_weights = weights[5]
     for start in range(0, depth, step):
-        values = mid[:, :, :, pl.ds(start, step)].astype(jnp.float32)
-        turned = swap_major(centred_unit(values.reshape(2 * hidden, step, width)))
         updates = []
-        for x in range(step):
-            operand = (turned[x] * out_gain).astype(jnp.bfloat16)
+        for x in range(start, start + step):
+            values = mid[:, :, x].astype(jnp.float32).reshape(2 * hidden, width)
+            operand = centred_unit(values, out_gain)
             projected = jnp.dot(out_weights, operand, preferred_element_type=jnp.float32)
-            updates.append((gates[start + x] * projected)[None])
+            updates.append((gates[x] * projected)[None])
         stacked = swap_major(jnp.concatenate(updates, axis=0))
         out_ref[:, pl.ds(start, step)] = stacked.astype(jnp.bfloat16)
 
     for swap in swaps:
         swap.wait_send()
-    for copy in (*edge_copies.values(), *tri_copies.values(), *relays):
+    for copies in (*first_copies, last_copies, *tri_copies):
+        for copy in copies.values():
+            copy.wait_send()
+    for copy in relays:
         copy.wait_send()
 
 
@@ -269,7 +306,7 @@
 ):
     half, depth, width = pair_act.shape
     hidden = left_proj.shape[1]
-    block = hidden // rows
+    part = hidden // rows // 2
     channels = 2 * half
     anywhere = pl.BlockSpec(memory_space=pl.ANY)
     local = pl.BlockSpec(memory_space=pltpu.VMEM)
@@ -277,27 +314,30 @@
     dma = pltpu.SemaphoreType.DMA
     return pl.pallas_call(
         functools.partial(fused_kernel, rows),
-        out_shape=jax.ShapeDtypeStruct(pair_act.shape, bf16),
+        out_shape=pltpu.VMEM(pair_act.shape, bf16),
         in_specs=[anywhere, local] + [anywhere] * 5 + [local, anywhere],
         out_specs=local,
         scratch_shapes=[
-            pltpu.VMEM((2, half, depth, width), bf16),
+            pltpu.VMEM((half, depth, width), bf16),
+            pltpu.VMEM((2, depth, half, width), bf16),
             pltpu.VMEM((2, 2, half, width), jnp.float32),
-            pltpu.VMEM((6 * hidden, channels), bf16),
+            pltpu.VMEM((6, hidden, channels), bf16),
+            pltpu.VMEM((2, 2 * hidden, channels), bf16),
             pltpu.VMEM((depth, channels, width), bf16),
             pltpu.VMEM((depth, hidden, width), jnp.float32),
-            pltpu.VMEM((rows, depth, 2 * block, width), bf16),
-            pltpu.VMEM((rows, depth, 2 * block, width), bf16),
-            pltpu.VMEM((2 * block, rows * depth, width), bf16),
-            pltpu.VMEM((rows, block, depth, width), bf16),
-            pltpu.VMEM((2, rows, block, depth, width), bf16),
+            pltpu.VMEM((2, rows, depth, 2 * part, width), bf16),
+            pltpu.VMEM((2, rows, depth, 2 * part, width), bf16),
+            pltpu.VMEM((2, 2 * part, rows * depth, width), bf16),
+            pltpu.VMEM((rows, 2, part, depth, width), bf16),
+            pltpu.VMEM((rows, 2, part, depth, width), bf16),
+            pltpu.VMEM((2, rows, depth, 2 * part, width), bf16),
             dma((7,)),
-            dma((2,)),
-            dma((2,)),
-            dma((rows,)),
-            dma((rows,)),
-            dma((rows,)),
-            dma((rows,)),
+            dma((3,)),
+            dma((3,)),
+            dma((3, rows)),
+            dma((3, rows)),
+            dma((2, rows)),
+            dma((2, rows)),
             dma((rows,)),
             dma((rows,)),
         ],

time: 32.6 us -> 30.5 us (0.936)
  the two profiles are of different devices: /device:TPU:1 before, /device:TPU:0 now
where the time goes in v2:
time: 30.5 us; the launch traced here: 30.4 us
  Pallas kernels  29.7 us (97%)
  local copies, waits for them, and re-layouts  0.71 us (2%)
    pallas_call x1, Pallas kernels, fused_device(): pl.pallas_call(functools.partial(fused_kernel, rows), out_shape=pltpu.VME...  29.7 us
    unnamed x1, local copies, waits for them, and re-layouts  0.71 us

profile of v2, /device:TPU:0, one launch (start us, length us, event | category | flops | bytes accessed | tf_op | source)
XLA Modules:
  0.0 30.4 jit_solution(10724451683567520775)
XLA Ops:
  0.0 29.7 %triangle.1 = bf16[64,16,128]{2,1,0:T(8,128)(2,1)S(1)} custom-call(bf16[64,16,128]{2,1,0:T(8,128)(2,1)} %act_ref.1, f32[1,64]{1,0:T(1,128)} %bitcast.14, bf16[64,128]{1,0:T(8,128)(2,1)} %bitcast.8, bf16[64,128]{1,0:T(8,128)(2,1)} %bitcast.9, bf16[64,128]{1,0:T(8,128)(2,1)} %bitcast.10, bf16[64,128]{1,0:T(8,128)(2,1)} %bitcast.11, bf16[64,128]{1,0:T(8,128)(2,1)} %bitcast.12, ...), custom_call_target="tpu_custom_call" | custom-call | tf_op jit(solution)/shard_map/triangle/pallas_call | solution.py:315
  29.7 0.7 %copy.11 = bf16[64,16,128]{2,1,0:T(8,128)(2,1)} copy(bf16[64,16,128]{2,1,0:T(8,128)(2,1)S(1)} %triangle.1) | data formatting | bytes 524288

commit v3 on v2

--- a/solution.py
+++ b/solution.py
@@ -118,6 +118,8 @@
     tri_recv,
     relay_send,
     relay_recv,
+    up_sem,
+    down_sem,
 ):
     me = lax.axis_index("row")
     core = lax.axis_index("ch")
@@ -138,9 +140,42 @@
     for load in loads:
         load.start()
     barrier = pltpu.get_barrier_semaphore()
-    pl.semaphore_signal(barrier, inc=1, device_id=partner, device_id_type=MESH)
-    for d in range(1, rows):
-        pl.semaphore_signal(barrier, inc=1, device_id={"row": peers[d]}, device_id_type=MESH)
+    side = lax.rem(me, 2)
+    across, above, below = me + 1 - 2 * side, me + 2, me - 2
+    has_above, has_below = me + 2 < rows, me >= 2
+
+    def greet(semaphore, device):
+        pl.semaphore_signal(semaphore, inc=1, device_id=device, device_id_type=MESH)
+
+    def pass_up():
+        @pl.when(has_below)
+        def _():
+            pl.semaphore_wait(up_sem, 1)
+
+        @pl.when(jnp.logical_and(has_below, has_above))
+        def _():
+            greet(up_sem, {"row": above})
+
+    def pass_down():
+        @pl.when(has_above)
+        def _():
+            pl.semaphore_wait(down_sem, 1)
+
+        @pl.when(jnp.logical_and(has_below, has_above))
+        def _():
+            greet(down_sem, {"row": below})
+
+    greet(barrier, partner)
+    greet(barrier, {"row": across})
+
+    @pl.when(has_above)
+    def _():
+        greet(barrier, {"row": above})
+
+    @pl.when(has_below)
+    def _():
+        greet(barrier, {"row": below})
+
     gains[core, 0] = spread_gain(gain_ref[...], width)
     gains[core, 1] = spread_gain(gain2_ref[...], width)
     loads[0].wait()
@@ -158,7 +193,16 @@
             device_id_type=MESH,
         )
 
-    pl.semaphore_wait(barrier, rows)
+    pl.semaphore_wait(barrier, 2 + has_above.astype(jnp.int32) + has_below.astype(jnp.int32))
+
+    @pl.when(jnp.logical_not(has_below))
+    def _():
+        greet(up_sem, {"row": above})
+
+    @pl.when(jnp.logical_not(has_above))
+    def _():
+        greet(down_sem, {"row": below})
+
     swaps = [
         to_partner(gains.at[core], 2),
         to_partner(act.at[core, halves[0]], 0),
@@ -166,6 +210,17 @@
     ]
     for swap in swaps:
         swap.start()
+
+    @pl.when(2 * me < rows)
+    def _():
+        pass_up()
+        pass_down()
+
+    @pl.when(2 * me >= rows)
+    def _():
+        pass_down()
+        pass_up()
+
     for load in loads[1:]:
         load.wait()
     for n in range(2):
@@ -340,6 +395,8 @@
             dma((2, rows)),
             dma((rows,)),
             dma((rows,)),
+            pltpu.SemaphoreType.REGULAR,
+            pltpu.SemaphoreType.REGULAR,
         ],
         compiler_params=pltpu.CompilerParams(collective_id=0, has_side_effects=True),
         name="triangle",
@@ -367,6 +424,8 @@
         and half == hidden
         and hidden % (8 * rows) == 0
         and depth % 16 == 0
+        and rows % 2 == 0
+        and rows >= 4
         and width % 128 == 0
     )
     if fits:

time: 30.5 us -> 31 us (1.016)
  the two profiles are of different devices: /device:TPU:0 before, /device:TPU:1 now
where the time goes in v3:
time: 31 us; the launch traced here: 30.9 us
  Pallas kernels  30.1 us (97%)
  local copies, waits for them, and re-layouts  0.71 us (2%)
    pallas_call x1, Pallas kernels, fused_device(): pl.pallas_call(functools.partial(fused_kernel, rows), out_shape=pltpu.VME...  30.1 us
    unnamed x1, local copies, waits for them, and re-layouts  0.71 us

profile of v3, /device:TPU:1, one launch (start us, length us, event | category | flops | bytes accessed | tf_op | source)
XLA Modules:
  0.0 30.9 jit_solution(17743135618645816074)
XLA Ops:
  0.0 30.1 %triangle.1 = bf16[64,16,128]{2,1,0:T(8,128)(2,1)S(1)} custom-call(bf16[64,16,128]{2,1,0:T(8,128)(2,1)} %act_ref.1, f32[1,64]{1,0:T(1,128)} %bitcast.14, bf16[64,128]{1,0:T(8,128)(2,1)} %bitcast.8, bf16[64,128]{1,0:T(8,128)(2,1)} %bitcast.9, bf16[64,128]{1,0:T(8,128)(2,1)} %bitcast.10, bf16[64,128]{1,0:T(8,128)(2,1)} %bitcast.11, bf16[64,128]{1,0:T(8,128)(2,1)} %bitcast.12, ...), custom_call_target="tpu_custom_call" | custom-call | tf_op jit(solution)/shard_map/triangle/pallas_call | solution.py:370
  30.1 0.7 %copy.11 = bf16[64,16,128]{2,1,0:T(8,128)(2,1)} copy(bf16[64,16,128]{2,1,0:T(8,128)(2,1)S(1)} %triangle.1) | data formatting | bytes 524288

commit v4 on v2

--- a/solution.py
+++ b/solution.py
@@ -109,6 +109,13 @@
     tri_out,
     tri_in,
     mid,
+    near_in,
+    near_edges,
+    part_sums,
+    part_out,
+    part_in,
+    near_out,
+    back_in,
     load_sem,
     pair_send,
     pair_recv,
@@ -118,6 +125,12 @@
     tri_recv,
     relay_send,
     relay_recv,
+    near_send,
+    near_recv,
+    part_send,
+    part_recv,
+    back_send,
+    back_recv,
 ):
     me = lax.axis_index("row")
     core = lax.axis_index("ch")
@@ -130,6 +143,13 @@
     sources = [lax.rem(me + rows - d, rows) for d in range(rows)]
     order = sorted(range(1, rows), key=lambda d: -min(d, rows - d))
     step = depth // 2
+    near = rows // 2
+    base = me // near * near
+    place = me - base
+    far_base = near - base
+    mates = [base + lax.rem(place + d, near) for d in range(near)]
+    mate_places = [lax.rem(place + d, near) for d in range(near)]
+    from_places = [lax.rem(place + near - d, near) for d in range(near)]
     halves = (pl.ds(0, step), pl.ds(step, step))
 
     loads = [pltpu.make_async_copy(act_ref, raw, load_sem.at[0])]
@@ -169,8 +189,8 @@
     for load in loads[1:]:
         load.wait()
     for n in range(2):
-        first = weights[n].astype(jnp.float32).reshape(rows, 2, part, 2 * half)
-        second = weights[n + 2].astype(jnp.float32).reshape(rows, 2, part, 2 * half)
+        first = weights[n].astype(jnp.float32).reshape(2, rows, part, 2 * half)
+        second = weights[n + 2].astype(jnp.float32).reshape(2, rows, part, 2 * half)
         joined = jnp.concatenate((first, second), axis=2)
         edge_weights[n] = joined.reshape(2 * hidden, 2 * half).astype(jnp.bfloat16)
 
@@ -191,7 +211,27 @@
         }
         for n in range(2)
     ]
-    last_copies = {d: edge_copy(2, outbox.at[1, peers[d]], inbox.at[1, me], d) for d in order}
+
+    def mate_copy(src, dst, sends, recvs, d):
+        return pltpu.make_async_remote_copy(
+            src_ref=src,
+            dst_ref=dst,
+            send_sem=sends.at[d],
+            recv_sem=recvs.at[d],
+            device_id={"row": mates[d]},
+            device_id_type=MESH,
+        )
+
+    near_copies = {
+        d: mate_copy(
+            outbox.at[1, pl.ds(2 * mate_places[d], 2)],
+            near_in.at[place],
+            near_send,
+            near_recv,
+            d,
+        )
+        for d in range(1, near)
+    }
 
     swaps[0].wait_recv()
     in_gain = gains[:, 0].reshape(2 * half, width)
@@ -204,79 +244,115 @@
             normed[x] = operand
             lifted = jnp.dot(lift_weights, operand, preferred_element_type=jnp.float32)
             both = jax.nn.sigmoid(lifted[2 * hidden :]) * lifted[: 2 * hidden]
-            both = both.reshape(rows, 2, 2 * part, width).astype(jnp.bfloat16)
-            outbox[0, :, x] = both[:, 0]
-            outbox[1, :, x] = both[:, 1]
+            both = both.reshape(2, rows, 2 * part, width).astype(jnp.bfloat16)
+            outbox[0, :, x] = both[0]
+            outbox[1, :, x] = both[1]
+        if n == 1:
+            for copy in near_copies.values():
+                copy.start()
         for d in order:
             first_copies[n][d].start()
-    for d in order:
-        last_copies[d].start()
-
-    def take_edges(n, box, source):
+
+    def take_edges(box, source):
         turned = swap_major(box.astype(jnp.float32)).astype(jnp.bfloat16)
-        edges[n, :, pl.ds(pl.multiple_of(source * depth, depth), depth)] = turned
-
-    for n in range(2):
-        take_edges(n, outbox[n, me], me)
+        edges[:, pl.ds(pl.multiple_of(source * depth, depth), depth)] = turned
+
+    def take_near(boxes, source):
+        for n in range(2):
+            turned = swap_major(boxes[n].astype(jnp.float32)).astype(jnp.bfloat16)
+            near_edges[n, :, pl.ds(pl.multiple_of(source * depth, depth), depth)] = turned
+
+    take_edges(outbox[0, me], me)
+    take_near(outbox.at[1, pl.ds(2 * place, 2)], place)
     gate_weights = weights[4]
     for x in range(depth):
         gates[x] = jax.nn.sigmoid(
             jnp.dot(gate_weights, normed[x], preferred_element_type=jnp.float32)
         )
 
-    def tri_copy(n, d):
-        return pltpu.make_async_remote_copy(
-            src_ref=tri_out.at[peers[d], n],
-            dst_ref=tri_in.at[me, n],
-            send_sem=tri_send.at[n, d],
-            recv_sem=tri_recv.at[n, d],
+    def contract(first, second):
+        return lax.dot_general(
+            first, second, (((0,), (0,)), ((), ())), preferred_element_type=jnp.float32
+        )
+
+    for d in range(1, near):
+        near_copies[d].wait_recv()
+        take_near(near_in.at[from_places[d]], from_places[d])
+    for n in range(2):
+        for h in range(part):
+            partial = contract(near_edges[n, h], near_edges[n, part + h])
+            part_sums[:, n * part + h] = partial.reshape(2, near * depth, width)
+    part_out[...] = part_sums[far_base // near].astype(jnp.bfloat16)
+    opposite = pltpu.make_async_remote_copy(
+        src_ref=part_out,
+        dst_ref=part_in,
+        send_sem=part_send.at[0],
+        recv_sem=part_recv.at[0],
+        device_id={"row": far_base + place},
+        device_id_type=MESH,
+    )
+    opposite.start()
+
+    tri_copies = {
+        d: pltpu.make_async_remote_copy(
+            src_ref=tri_out.at[peers[d]],
+            dst_ref=tri_in.at[me],
+            send_sem=tri_send.at[d],
+            recv_sem=tri_recv.at[d],
             device_id={"row": peers[d]},
             device_id_type=MESH,
         )
-
-    tri_copies = [{d: tri_copy(n, d) for d in order} for n in range(2)]
-    for n in range(2):
-        for d in order:
-            if n == 0:
-                first_copies[0][d].wait_recv()
-                first_copies[1][d].wait_recv()
-            else:
-                last_copies[d].wait_recv()
-            take_edges(n, inbox[n, sources[d]], sources[d])
-        for h in range(part):
-            tri_sum = lax.dot_general(
-                edges[n, h],
-                edges[n, part + h],
-                (((0,), (0,)), ((), ())),
-                preferred_element_type=jnp.float32,
+        for d in order
+    }
+    for d in order:
+        first_copies[0][d].wait_recv()
+        first_copies[1][d].wait_recv()
+        take_edges(inbox[0, sources[d]], sources[d])
+    for h in range(part):
+        tri_sum = contract(edges[h], edges[part + h])
+        tri_out[:, h] = tri_sum.astype(jnp.bfloat16).reshape(rows, depth, width)
+    for d in order:
+        tri_copies[d].start()
+
+    opposite.wait_recv()
+    for h in range(2 * part):
+        full = part_sums[base // near, h] + part_in[h].astype(jnp.float32)
+        near_out[:, h] = full.astype(jnp.bfloat16).reshape(near, depth, width)
+    back_copies = {
+        d: mate_copy(near_out.at[mate_places[d]], back_in.at[place], back_send, back_recv, d)
+        for d in range(1, near)
+    }
+    for copy in back_copies.values():
+        copy.start()
+
+    relays = []
+
+    def pass_mid(block, group, source):
+        block = block.astype(jnp.float32).reshape(2 * part, depth, width)
+        mid[core, group, source] = swap_major(block).astype(jnp.bfloat16)
+        n = len(relays)
+        relays.append(
+            pltpu.make_async_remote_copy(
+                src_ref=mid.at[core, group, source],
+                dst_ref=mid.at[core, group, source],
+                send_sem=relay_send.at[n],
+                recv_sem=relay_recv.at[n],
+                device_id=partner,
+                device_id_type=MESH,
             )
-            tri_out[:, n, h] = tri_sum.astype(jnp.bfloat16).reshape(rows, depth, width)
-        for d in order:
-            tri_copies[n][d].start()
-
-    def relay(source, d):
-        return pltpu.make_async_remote_copy(
-            src_ref=mid.at[core, source],
-            dst_ref=mid.at[core, source],
-            send_sem=relay_send.at[d],
-            recv_sem=relay_recv.at[d],
-            device_id=partner,
-            device_id_type=MESH,
-        )
-
-    def take_mid(block, source):
-        block = block.astype(jnp.float32).reshape(2 * part, depth, width)
-        mid[core, source] = swap_major(block).astype(jnp.bfloat16)
-
-    take_mid(tri_out[me], me)
-    relays = [relay(me, 0)]
-    relays[0].start()
+        )
+        relays[n].start()
+
+    pass_mid(near_out[place], 1, place)
+    for d in range(1, near):
+        back_copies[d].wait_recv()
+        pass_mid(back_in[from_places[d]], 1, from_places[d])
+    tri_in[me] = tri_out[me]
     for d in order:
-        for n in range(2):
-            tri_copies[n][d].wait_recv()
-        take_mid(tri_in[sources[d]], sources[d])
-        relays.append(relay(sources[d], d))
-        relays[-1].start()
+        tri_copies[d].wait_recv()
+    for d in range(near):
+        source = from_places[d]
+        pass_mid(tri_in[pl.ds(2 * source, 2)], 0, source)
     for copy in relays:
         copy.wait_recv()
 
@@ -285,7 +361,7 @@
     for start in range(0, depth, step):
         updates = []
         for x in range(start, start + step):
-            values = mid[:, :, x].astype(jnp.float32).reshape(2 * hidden, width)
+            values = mid[:, :, :, x].astype(jnp.float32).reshape(2 * hidden, width)
             operand = centred_unit(values, out_gain)
             projected = jnp.dot(out_weights, operand, preferred_element_type=jnp.float32)
             updates.append((gates[x] * projected)[None])
@@ -294,7 +370,8 @@
 
     for swap in swaps:
         swap.wait_send()
-    for copies in (*first_copies, last_copies, *tri_copies):
+    opposite.wait_send()
+    for copies in (*first_copies, near_copies, back_copies, tri_copies):
         for copy in copies.values():
             copy.wait_send()
     for copy in relays:
@@ -308,6 +385,7 @@
     hidden = left_proj.shape[1]
     part = hidden // rows // 2
     channels = 2 * half
+    near = rows // 2
     anywhere = pl.BlockSpec(memory_space=pl.ANY)
     local = pl.BlockSpec(memory_space=pltpu.VMEM)
     bf16 = jnp.bfloat16
@@ -326,20 +404,33 @@
             pltpu.VMEM((depth, channels, width), bf16),
             pltpu.VMEM((depth, hidden, width), jnp.float32),
             pltpu.VMEM((2, rows, depth, 2 * part, width), bf16),
-            pltpu.VMEM((2, rows, depth, 2 * part, width), bf16),
-            pltpu.VMEM((2, 2 * part, rows * depth, width), bf16),
-            pltpu.VMEM((rows, 2, part, depth, width), bf16),
-            pltpu.VMEM((rows, 2, part, depth, width), bf16),
-            pltpu.VMEM((2, rows, depth, 2 * part, width), bf16),
+            pltpu.VMEM((1, rows, depth, 2 * part, width), bf16),
+            pltpu.VMEM((2 * part, rows * depth, width), bf16),
+            pltpu.VMEM((rows, part, depth, width), bf16),
+            pltpu.VMEM((rows, part, depth, width), bf16),
+            pltpu.VMEM((2, 2, near, depth, 2 * part, width), bf16),
+            pltpu.VMEM((near, 2, depth, 2 * part, width), bf16),
+            pltpu.VMEM((2, 2 * part, near * depth, width), bf16),
+            pltpu.VMEM((2, 2 * part, near * depth, width), jnp.float32),
+            pltpu.VMEM((2 * part, near * depth, width), bf16),
+            pltpu.VMEM((2 * part, near * depth, width), bf16),
+            pltpu.VMEM((near, 2 * part, depth, width), bf16),
+            pltpu.VMEM((near, 2 * part, depth, width), bf16),
             dma((7,)),
             dma((3,)),
             dma((3,)),
             dma((3, rows)),
             dma((3, rows)),
-            dma((2, rows)),
-            dma((2, rows)),
             dma((rows,)),
             dma((rows,)),
+            dma((rows,)),
+            dma((rows,)),
+            dma((near,)),
+            dma((near,)),
+            dma((1,)),
+            dma((1,)),
+            dma((near,)),
+            dma((near,)),
         ],
         compiler_params=pltpu.CompilerParams(collective_id=0, has_side_effects=True),
         name="triangle",
@@ -367,6 +458,7 @@
         and half == hidden
         and hidden % (8 * rows) == 0
         and depth % 16 == 0
+        and rows % 2 == 0
         and width % 128 == 0
     )
     if fits:

time: 30.5 us -> 30.8 us (level)
  the two profiles are of different devices: /device:TPU:0 before, /device:TPU:1 now
where the time goes in v4:
time: 30.8 us; the launch traced here: 30.6 us
  Pallas kernels  29.9 us (97%)
  local copies, waits for them, and re-layouts  0.71 us (2%)
    pallas_call x1, Pallas kernels, fused_device(): pl.pallas_call(functools.partial(fused_kernel, rows), out_shape=pltpu.VME...  29.9 us
    unnamed x1, local copies, waits for them, and re-layouts  0.71 us

profile of v4, /device:TPU:1, one launch (start us, length us, event | category | flops | bytes accessed | tf_op | source)
XLA Modules:
  0.0 30.6 jit_solution(15138155866276621057)
XLA Ops:
  0.0 29.9 %triangle.1 = bf16[64,16,128]{2,1,0:T(8,128)(2,1)S(1)} custom-call(bf16[64,16,128]{2,1,0:T(8,128)(2,1)} %act_ref.1, f32[1,64]{1,0:T(1,128)} %bitcast.14, bf16[64,128]{1,0:T(8,128)(2,1)} %bitcast.8, bf16[64,128]{1,0:T(8,128)(2,1)} %bitcast.9, bf16[64,128]{1,0:T(8,128)(2,1)} %bitcast.10, bf16[64,128]{1,0:T(8,128)(2,1)} %bitcast.11, bf16[64,128]{1,0:T(8,128)(2,1)} %bitcast.12, ...), custom_call_target="tpu_custom_call" | custom-call | tf_op jit(solution)/shard_map/triangle/pallas_call | solution.py:393
  29.9 0.7 %copy.11 = bf16[64,16,128]{2,1,0:T(8,128)(2,1)} copy(bf16[64,16,128]{2,1,0:T(8,128)(2,1)S(1)} %triangle.1) | data formatting | bytes 524288

commit v5 on v4

--- a/solution.py
+++ b/solution.py
@@ -206,10 +206,10 @@
 
     first_copies = [
         {
-            d: edge_copy(n, outbox.at[0, peers[d], halves[n]], inbox.at[0, me, halves[n]], d)
+            d: edge_copy(n, outbox.at[0, peers[d]], inbox.at[0, me], d)
             for d in order
         }
-        for n in range(2)
+        for n in range(1)
     ]
 
     def mate_copy(src, dst, sends, recvs, d):
@@ -247,11 +247,11 @@
             both = both.reshape(2, rows, 2 * part, width).astype(jnp.bfloat16)
             outbox[0, :, x] = both[0]
             outbox[1, :, x] = both[1]
-        if n == 1:
-            for copy in near_copies.values():
-                copy.start()
-        for d in order:
-            first_copies[n][d].start()
+
+    for copy in near_copies.values():
+        copy.start()
+    for d in order:
+        first_copies[0][d].start()
 
     def take_edges(box, source):
         turned = swap_major(box.astype(jnp.float32)).astype(jnp.bfloat16)
@@ -306,7 +306,6 @@
     }
     for d in order:
         first_copies[0][d].wait_recv()
-        first_copies[1][d].wait_recv()
         take_edges(inbox[0, sources[d]], sources[d])
     for h in range(part):
         tri_sum = contract(edges[h], edges[part + h])

time: 30.8 us -> 29.6 us (0.961)
  Pallas kernels: 29.9 us -> 28.6 us
    pallas_call x1, Pallas kernels: 29.9 us -> 28.6 us  [fused_device(): pl.pallas_call(functools.partial(fused_kernel, rows), out_shape=pltpu.VME...]
where the time goes in v5:
time: 29.6 us; the launch traced here: 29.3 us
  Pallas kernels  28.6 us (97%)
  local copies, waits for them, and re-layouts  0.71 us (2%)
    pallas_call x1, Pallas kernels, fused_device(): pl.pallas_call(functools.partial(fused_kernel, rows), out_shape=pltpu.VME...  28.6 us
    unnamed x1, local copies, waits for them, and re-layouts  0.71 us

profile of v5, /device:TPU:1, one launch (start us, length us, event | category | flops | bytes accessed | tf_op | source)
XLA Modules:
  0.0 29.3 jit_solution(15608756947188239816)
XLA Ops:
  0.0 28.6 %triangle.1 = bf16[64,16,128]{2,1,0:T(8,128)(2,1)S(1)} custom-call(bf16[64,16,128]{2,1,0:T(8,128)(2,1)} %act_ref.1, f32[1,64]{1,0:T(1,128)} %bitcast.14, bf16[64,128]{1,0:T(8,128)(2,1)} %bitcast.8, bf16[64,128]{1,0:T(8,128)(2,1)} %bitcast.9, bf16[64,128]{1,0:T(8,128)(2,1)} %bitcast.10, bf16[64,128]{1,0:T(8,128)(2,1)} %bitcast.11, bf16[64,128]{1,0:T(8,128)(2,1)} %bitcast.12, ...), custom_call_target="tpu_custom_call" | custom-call | tf_op jit(solution)/shard_map/triangle/pallas_call | solution.py:392
  28.6 0.7 %copy.11 = bf16[64,16,128]{2,1,0:T(8,128)(2,1)} copy(bf16[64,16,128]{2,1,0:T(8,128)(2,1)S(1)} %triangle.1) | data formatting | bytes 524288
